TPU v7x, 256 devices: a 4x2x16 block of a 4x16x16 slice. The times are simulated.
256 devices in a mesh: arm: 2 (over y), snp: 128 (over z, x, core).
Axes of the slice: x: 4, y: 2, z: 16, core: 2. Of those that a mesh axis runs over, the one named last changes fastest.
The devices are a block of a 4x16x16 slice.
Arguments:
- genotypes: int32 [32768, 1024], P(('arm', 'snp')), parts along dimension 0, may hold values from -2147483648 to 2147483647, as said below
- positions: int32 [32768], P(('arm', 'snp')), parts along dimension 0, may hold values from 2001303 to 28673152, as said below
Outputs:
- linkage: float32 [32768, 1664], P(('arm', 'snp')), parts along dimension 0
There are 2 independent parts, one for each index of `arm`. A program takes and returns all parts, laid end to end along the dimension named above; each array names one. Nothing has to cross between parts.
Inputs may be any that keep to these rules, and one draw needn't show every extreme that they name: `genotypes`: each word holds 16 two-bit codes: the call of sample s sits in bits 2 * (s // 1024) and 2 * (s // 1024) + 1 of word s mod 1024; codes 0, 1, 2 count alternate alleles and code 3 marks a missing call. `positions`: strictly increasing; consecutive SNPs lie 1303 or more base pairs apart.
All inputs are finite; a program needn't handle non-finite values.
Results may differ from a plain program's by a relative error of at most 0.0031.
Values may be sent and summed in bfloat16 or wider, within the bound.
A program may use at most 128 MiB of HBM per device.

v0:
```python
import functools

import jax
import jax.numpy as jnp
from jax import lax
from jax.experimental import pallas as pl
from jax.experimental.pallas import tpu as pltpu
from jax.sharding import PartitionSpec as P

REACH = 6
BAND_BP = 1000000
COLS = 4
LANES = 128
CODES = 16
RL, LR, ZRL, ZLR, OWN = range(5)
MESH = pl.DeviceIdType.MESH
I16 = jnp.int16
OWNERS = ((1, (0, 3)), (-1, (2, 3)), (2, (0, 1)), (-2, (0, 1)), (3, (2, 3)), (-3, (0, 3)))


def any_of(col, cols):
    hit = col == cols[0]
    for c in cols[1:]:
        hit = hit | (col == c)
    return hit


def lookup(half, bit, v0, v1, v2, zero):
    high = 2 << bit
    low_set = (half & I16(1 << bit)) != I16(0)
    high_set = (half & I16(high if high < 32768 else -32768)) != I16(0)
    return jnp.where(high_set, jnp.where(low_set, zero, v2), jnp.where(low_set, v1, v0))


def values_of(missing, dosage, samples):
    tally = samples - missing.astype(jnp.float32)
    allele = (dosage.astype(jnp.float32) + 1.0) / (2.0 * tally + 2.0)
    spread = lax.rsqrt(2.0 * allele * (1.0 - allele))
    return [(code - 2.0 * allele) * spread for code in (0.0, 1.0, 2.0)]


def kernel(devices, geno, pos, out, buf, xbuf, own_t, panel, acc, part, tab, place_of,
           lane_tab, meta_out, meta_in, mir_out, mir_in,
           load_sem, x_send, fwd_send, fwd2_send, arrive, meta_send, meta_recv, sib_send,
           part_send, part_recv, mir_send, mir_recv):
    rows = pos.shape[1]
    words = geno.shape[1]
    parts = words // (2 * LANES)
    samples = float(words * CODES)
    me = lax.axis_index("snp")
    chips = devices // 2
    core = lax.rem(me, 2)
    chip = me // 2
    col = lax.rem(chip, COLS)
    base = chip - col

    def rel(offset):
        return lax.rem(chip + offset + chips, chips)

    left = base + lax.rem(col + COLS - 1, COLS)
    right = base + lax.rem(col + 1, COLS)
    sibling = me + 1 - 2 * core

    def core_of(c, k):
        return {"snp": c * 2 + k}

    loads = []
    for e in range(2):
        half = core if e == 0 else 1 - core
        for j in range(parts):
            lane = pl.multiple_of((half * parts + j) * LANES, LANES)
            dst = buf.at[OWN, 0, j] if e == 0 else xbuf.at[j]
            loads.append(pltpu.make_async_copy(geno.at[:, pl.ds(lane, LANES)], dst, load_sem.at[e, j]))
            loads[-1].start()

    def own_piece(e, j):
        return buf.at[OWN, 0, j] if e == 0 else xbuf.at[j]

    barrier = pltpu.get_barrier_semaphore()
    partners = [left, right] + [rel(o) for o in (COLS, -COLS, 1, -1, 2, -2, 3, -3)]
    for c in partners:
        for k in range(2):
            pl.semaphore_signal(barrier, inc=1, device_id=core_of(c, k), device_id_type=MESH)
    pl.semaphore_signal(barrier, inc=1, device_id={"snp": sibling}, device_id_type=MESH)
    for copy in loads:
        copy.wait()
    pl.semaphore_wait(barrier, 2 * len(partners) + 1)

    sends_left = col >= 1
    sends_right = (col == 0) | (col == 3)
    uses_rl = col >= 1
    uses_lr = col <= 2
    dz_rl = jnp.where(col == 3, -1, 1)
    dz_lr = jnp.where(col == 0, 1, -1)
    off_rl = jnp.where(col == 3, -2, 1)
    off_lr = jnp.where(col == 0, 3, jnp.where(col == 1, -1, -2))
    off_zrl = off_rl - COLS * dz_rl
    off_zlr = off_lr - COLS * dz_lr

    def offset_of(s):
        return jnp.where(s == RL, off_rl, jnp.where(s == LR, off_lr, jnp.where(s == ZRL, off_zrl, off_zlr)))

    def uses(s):
        return jnp.where((s == RL) | (s == ZRL), col >= 1, col <= 2)

    def hop(src, send_sem, s, e, j, target):
        return pltpu.make_async_remote_copy(
            src_ref=src, dst_ref=buf.at[s, e, j], send_sem=send_sem, recv_sem=arrive.at[s, e, j],
            device_id=target, device_id_type=MESH)

    def x_hop(e, j, way):
        target = core_of(left if way == RL else right, core if e == 0 else 1 - core)
        return hop(own_piece(e, j), x_send.at[way, e, j], way, e, j, target)

    for way, sends in ((RL, sends_left), (LR, sends_right)):
        @pl.when(sends)
        def _(way=way):
            for j in range(parts):
                for e in range(2):
                    x_hop(e, j, way).start()

    def to_sibling(j):
        return hop(xbuf.at[j], sib_send.at[j], OWN, 1, j, {"snp": sibling})

    for j in range(parts):
        to_sibling(j).start()

    missing = jnp.zeros((rows, LANES), jnp.int32)
    dosage = jnp.zeros((rows, LANES), jnp.int32)
    for e in range(2):
        for j in range(parts):
            word = own_piece(e, j)[...]
            low = word & 0x55555555
            high = lax.shift_right_logical(word, 1) & 0x55555555
            gone = lax.population_count(low & high)
            missing = missing + gone
            dosage = dosage + lax.population_count(low) + 2 * lax.population_count(high) - 3 * gone
    counts = []
    for x in (missing, dosage):
        total = jnp.broadcast_to(jnp.sum(x, axis=1, keepdims=True), (rows, LANES))
        counts.append(total.T[0:1])
    meta_out[0:1] = pos[...]
    meta_out[1:2] = counts[0]
    meta_out[2:3] = counts[1]
    meta_out[3:8] = jnp.zeros((5, LANES), jnp.int32)

    def meta_copy(offset, e):
        k = core if e == 0 else 1 - core
        return pltpu.make_async_remote_copy(
            src_ref=meta_out, dst_ref=meta_in.at[3 - offset, e], send_sem=meta_send.at[3 + offset, e],
            recv_sem=meta_recv.at[3 - offset, e],
            device_id={"snp": sibling} if offset == 0 else core_of(rel(offset), k), device_id_type=MESH)

    meta_copy(0, 1).start()
    for offset, cols in OWNERS:
        @pl.when(any_of(col, cols))
        def _(offset=offset):
            for e in range(2):
                meta_copy(offset, e).start()

    def fill_tables(s, e, counts8):
        columns = [jnp.broadcast_to(counts8.T[:, i:i + 1], (rows, LANES)) for i in range(3)]
        place_of[s, e] = columns[0]
        for i, v in enumerate(values_of(columns[1], columns[2], samples)):
            tab[s, e, i] = v.astype(jnp.bfloat16)

    def batch(s, j, first):
        for e in range(2):
            word = buf[s, e, j]
            halves = word.astype(I16), lax.shift_right_logical(word, 16).astype(I16)
            v0, v1, v2 = (tab[s, e, i] for i in range(3))
            zero = jnp.zeros_like(v0)
            for q in range(CODES):
                panel[e * rows:(e + 1) * rows, q * LANES:(q + 1) * LANES] = lookup(
                    halves[q // 8], 2 * (q % 8), v0, v1, v2, zero)
        product = lax.dot_general(panel[...], own_t[j], (((1,), (0,)), ((), ())),
                                  preferred_element_type=jnp.float32)
        for e in range(2):
            for c in range(2):
                tile = product[e * rows:(e + 1) * rows, c * LANES:(c + 1) * LANES]
                acc[s, e, c] = jnp.where(first, tile, acc[s, e, c] + tile)

    pltpu.make_async_remote_copy(
        src_ref=meta_out, dst_ref=meta_in.at[3, 1], send_sem=meta_send.at[3, 1], recv_sem=meta_recv.at[3, 1],
        device_id={"snp": sibling}, device_id_type=MESH).wait_recv()
    for e in range(2):
        counts8 = meta_out[...] if e == 0 else meta_in[3, 1]
        fill_tables(OWN, e, counts8)
        for i, v in enumerate(values_of(counts8[1:2], counts8[2:3], samples)):
            lane_tab[e, i] = jnp.broadcast_to(v, (rows, LANES)).astype(jnp.bfloat16)

    def own_step(j, carry):
        hop(xbuf.at[j], sib_send.at[j], OWN, 1, j, {"snp": sibling}).wait_recv()
        for e in range(2):
            word = buf[OWN, e, j].T
            halves = word.astype(I16), lax.shift_right_logical(word, 16).astype(I16)
            v0, v1, v2 = (lane_tab[e, i] for i in range(3))
            zero = jnp.zeros_like(v0)
            for q in range(CODES):
                own_t[j, q * LANES:(q + 1) * LANES, e * rows:(e + 1) * rows] = lookup(
                    halves[q // 8], 2 * (q % 8), v0, v1, v2, zero)
        batch(OWN, j, j == 0)
        return carry

    lax.fori_loop(0, parts, own_step, 0)

    def part_copy(s, e):
        return pltpu.make_async_remote_copy(
            src_ref=acc.at[s, e, 1], dst_ref=part.at[s, 1 - e], send_sem=part_send.at[s, e],
            recv_sem=part_recv.at[s, 1 - e], device_id={"snp": sibling}, device_id_type=MESH)

    def part_arrived(s, e):
        pltpu.make_async_remote_copy(
            src_ref=acc.at[s, e, 1], dst_ref=part.at[s, e], send_sem=part_send.at[s, e],
            recv_sem=part_recv.at[s, e], device_id={"snp": sibling}, device_id_type=MESH).wait_recv()

    for e in range(2):
        part_copy(OWN, e).start()

    def table_step(s, carry):
        @pl.when(uses(s))
        def _():
            slot = offset_of(s) + 3
            for e in range(2):
                pltpu.make_async_remote_copy(
                    src_ref=meta_out, dst_ref=meta_in.at[slot, e], send_sem=meta_send.at[slot, e],
                    recv_sem=meta_recv.at[slot, e], device_id={"snp": sibling},
                    device_id_type=MESH).wait_recv()
                fill_tables(s, e, meta_in[slot, e])
        return carry

    lax.fori_loop(0, 4, table_step, 0)

    rl_target = jnp.where(col == 0, left, rel(COLS * dz_rl))
    rl_slot = jnp.where(col == 0, RL, ZRL)

    def fwd_rl(e, j):
        return hop(buf.at[RL, e, j], fwd_send.at[RL, e, j], rl_slot, e, j, core_of(rl_target, core))

    def fwd_lr(e, j):
        return hop(buf.at[LR, e, j], fwd_send.at[LR, e, j], ZLR, e, j, core_of(rel(COLS * dz_lr), core))

    def fwd_lr_on(e, j):
        return hop(buf.at[LR, e, j], fwd2_send.at[e, j], LR, e, j, core_of(right, core))

    def arrived(s, e, j):
        hop(buf.at[s, e, j], fwd_send.at[RL, e, j], s, e, j, {"snp": sibling}).wait_recv()

    def step(t, carry):
        @pl.when(t < parts)
        def _():
            for e in range(2):
                arrived(RL, e, t)
                fwd_rl(e, t).start()

                @pl.when(uses_lr)
                def _(e=e):
                    arrived(LR, e, t)

                    @pl.when(col == 1)
                    def _():
                        fwd_lr_on(e, t).start()
                    fwd_lr(e, t).start()

        def stream(s, inner):
            j = jnp.where(s >= ZRL, t - 1, t)

            @pl.when(uses(s) & (j >= 0) & (j < parts))
            def _():
                @pl.when(s >= ZRL)
                def _():
                    for e in range(2):
                        arrived(s, e, j)
                batch(s, j, j == 0)

                @pl.when(j == parts - 1)
                def _():
                    for e in range(2):
                        part_copy(s, e).start()
            return inner

        lax.fori_loop(0, 4, stream, 0)
        return carry

    lax.fori_loop(0, parts + 1, step, 0)

    def put(tile, at):
        @pl.when((at >= 0) & (at <= 2 * REACH))
        def _():
            out[:, pl.ds(pl.multiple_of(at * LANES, LANES), LANES)] = tile

    def finished(s, e):
        part_arrived(s, e)
        tile = (acc[s, e, 0] + part[s, e]) / samples
        near = jnp.abs(place_of[s, e] - pos[...]) <= BAND_BP
        return jnp.where(near, tile, jnp.zeros_like(tile))

    def mirror_copy(s, e, offset):
        k = core if e == 0 else 1 - core
        return pltpu.make_async_remote_copy(
            src_ref=mir_out.at[s, e], dst_ref=mir_in.at[3 - offset, e], send_sem=mir_send.at[s, e],
            recv_sem=mir_recv.at[3 - offset, e], device_id=core_of(rel(offset), k), device_id_type=MESH)

    def column_of(offset, e):
        k = core if e == 0 else 1 - core
        return 2 * (offset + 3) + k - core

    def finish_step(s, carry):
        @pl.when(uses(s))
        def _():
            offset = offset_of(s)
            for e in range(2):
                tile = finished(s, e)
                mir_out[s, e] = tile.astype(jnp.bfloat16)
                mirror_copy(s, e, offset).start()
                put(tile.T, column_of(offset, e))
        return carry

    lax.fori_loop(0, 4, finish_step, 0)
    for e in range(2):
        put(finished(OWN, e).T, column_of(0, e))

    for offset, cols in OWNERS:
        @pl.when(any_of(col, cols))
        def _(offset=offset):
            for e in range(2):
                pltpu.make_async_remote_copy(
                    src_ref=mir_out.at[0, e], dst_ref=mir_in.at[3 + offset, e], send_sem=mir_send.at[0, e],
                    recv_sem=mir_recv.at[3 + offset, e], device_id={"snp": sibling},
                    device_id_type=MESH).wait_recv()
                put(mir_in[3 + offset, e].astype(jnp.float32), column_of(offset, e))

    for way, sends in ((RL, sends_left), (LR, sends_right)):
        @pl.when(sends)
        def _(way=way):
            for j in range(parts):
                for e in range(2):
                    x_hop(e, j, way).wait_send()
    for j in range(parts):
        to_sibling(j).wait_send()
        for e in range(2):
            fwd_rl(e, j).wait_send()

    @pl.when(uses_lr)
    def _():
        for j in range(parts):
            for e in range(2):
                fwd_lr(e, j).wait_send()

    @pl.when(col == 1)
    def _():
        for j in range(parts):
            for e in range(2):
                fwd_lr_on(e, j).wait_send()
    meta_copy(0, 1).wait_send()
    for offset, cols in OWNERS:
        @pl.when(any_of(col, cols))
        def _(offset=offset):
            for e in range(2):
                meta_copy(offset, e).wait_send()
    for e in range(2):
        part_copy(OWN, e).wait_send()

    def drain(s, carry):
        @pl.when(uses(s))
        def _():
            for e in range(2):
                part_copy(s, e).wait_send()
                mirror_copy(s, e, offset_of(s)).wait_send()
        return carry

    lax.fori_loop(0, 4, drain, 0)


def per_device(genotypes, positions):
    devices = lax.axis_size("snp")
    rows, words = genotypes.shape
    parts = words // (2 * LANES)
    piece = (rows, LANES)
    dma = pltpu.SemaphoreType.DMA
    return pl.pallas_call(
        functools.partial(kernel, devices),
        out_shape=jax.ShapeDtypeStruct((rows, (2 * REACH + 1) * LANES), jnp.float32),
        in_specs=[pl.BlockSpec(memory_space=pltpu.HBM), pl.BlockSpec(memory_space=pltpu.VMEM)],
        out_specs=pl.BlockSpec(memory_space=pltpu.VMEM),
        scratch_shapes=[
            pltpu.VMEM((5, 2, parts) + piece, jnp.int32),
            pltpu.VMEM((parts,) + piece, jnp.int32),
            pltpu.VMEM((parts, CODES * LANES, 2 * rows), jnp.bfloat16),
            pltpu.VMEM((2 * rows, CODES * LANES), jnp.bfloat16),
            pltpu.VMEM((5, 2, 2) + piece, jnp.float32),
            pltpu.VMEM((5, 2) + piece, jnp.float32),
            pltpu.VMEM((5, 2, 3) + piece, jnp.bfloat16),
            pltpu.VMEM((5, 2) + piece, jnp.int32),
            pltpu.VMEM((2, 3) + piece, jnp.bfloat16),
            pltpu.VMEM((8, LANES), jnp.int32),
            pltpu.VMEM((7, 2, 8, LANES), jnp.int32),
            pltpu.VMEM((4, 2) + piece, jnp.bfloat16),
            pltpu.VMEM((7, 2) + piece, jnp.bfloat16),
            dma((2, parts)),
            dma((2, 2, parts)),
            dma((2, 2, parts)),
            dma((2, parts)),
            dma((5, 2, parts)),
            dma((7, 2)),
            dma((7, 2)),
            dma((parts,)),
            dma((5, 2)),
            dma((5, 2)),
            dma((4, 2)),
            dma((7, 2)),
        ],
        compiler_params=pltpu.CompilerParams(
            collective_id=0, has_side_effects=True, vmem_limit_bytes=40 * 1024 * 1024
        ),
    )(genotypes, positions.reshape(1, rows))


def solution(mesh):
    return jax.shard_map(
        per_device,
        mesh=mesh,
        in_specs=(P(("arm", "snp"), None), P(("arm", "snp"))),
        out_specs=P(("arm", "snp"), None),
        check_vma=False,
    )
```

profile of v0, /device:TPU:33, one launch (start us, length us, event | category | flops | bytes accessed | tf_op | source)
XLA Modules:
  0.0 72.9 jit_solution(4950848360033279341)
XLA Ops:
  0.0 0.0 copy-start.1
  0.0 0.7 copy-done.1
  0.7 0.0 copy-start
  0.7 1.0 %copy-done = s32[128,1024]{1,0:T(8,128)S(1)} copy-done((s32[128,1024]{1,0:T(8,128)S(1)}, s32[128,1024]{1,0:T(8,128)}, u32[]{:S(2)}) %copy-start) | copy-done | bytes 524312
  1.7 70.2 %shard_map.28 = f32[128,1664]{1,0:T(8,128)S(1)} custom-call(s32[128,1024]{1,0:T(8,128)S(1)} %copy-done, s32[1,128]{1,0:T(1,128)S(1)} %bitcast.1), custom_call_target="tpu_custom_call" | custom-call | tf_op jit(solution)/shard_map/pallas_call | solution.py:381
  72.0 0.9 %copy.4 = f32[128,1664]{1,0:T(8,128)} copy(f32[128,1664]{1,0:T(8,128)S(1)} %shard_map.28) | data formatting | bytes 1703936
Async XLA Ops:
  0.0 0.7 copy-start.1
  0.7 1.0 %copy-start = (s32[128,1024]{1,0:T(8,128)S(1)}, s32[128,1024]{1,0:T(8,128)}, u32[]{:S(2)}) copy-start(s32[128,1024]{1,0:T(8,128)} %geno.1) | copy-start | bytes 1572868
where the time goes:
time: 73 us; the launch traced here: 72.9 us
  Pallas kernels  70.2 us (96%)
  local copies, waits for them, and re-layouts  2.6 us (4%)
    pallas_call x1, Pallas kernels, per_device(): pl.pallas_call(functools.partial(kernel, devices), out_shape=jax.ShapeDty...  70.2 us
    unnamed x5, local copies, waits for them, and re-layouts  2.6 us

commit v1 on v0

v1 whole, which is shorter than its diff:
```python
import functools

import jax
import jax.numpy as jnp
from jax import lax
from jax.experimental import pallas as pl
from jax.experimental.pallas import tpu as pltpu
from jax.sharding import PartitionSpec as P

REACH = 6
BAND_BP = 1000000
COLS = 4
LANES = 128
CODES = 16
RL, LR, ZRL, ZLR, OWN = range(5)
MESH = pl.DeviceIdType.MESH
I16 = jnp.int16
GROUP = 16
OWNERS = ((1, (0, 3)), (-1, (2, 3)), (2, (0, 1)), (-2, (0, 1)), (3, (2, 3)), (-3, (0, 3)))


def any_of(col, cols):
    hit = col == cols[0]
    for c in cols[1:]:
        hit = hit | (col == c)
    return hit


def lookup(half, bit, v0, v1, v2, zero):
    high = 2 << bit
    low_set = (half & I16(1 << bit)) != I16(0)
    high_set = (half & I16(high if high < 32768 else -32768)) != I16(0)
    return jnp.where(high_set, jnp.where(low_set, zero, v2), jnp.where(low_set, v1, v0))


def values_of(missing, dosage, samples):
    tally = samples - missing.astype(jnp.float32)
    allele = (dosage.astype(jnp.float32) + 1.0) / (2.0 * tally + 2.0)
    spread = lax.rsqrt(2.0 * allele * (1.0 - allele))
    return [(code - 2.0 * allele) * spread for code in (0.0, 1.0, 2.0)]


def kernel(devices, geno, pos_hbm, out, pos, buf, xbuf, own_t, panel, acc, part, tab, place_of,
           lane_tab, meta_out, meta_in, mir_out, mir_in,
           lane_val, late_sem, load_sem, pos_sem, x_send, fwd_send, fwd2_send, arrive, meta_send, meta_recv, sib_send,
           part_send, part_recv, mir_send, mir_recv):
    rows = pos_hbm.shape[1]
    words = geno.shape[1]
    parts = words // (2 * LANES)
    samples = float(words * CODES)
    me = lax.axis_index("snp")
    chips = devices // 2
    core = lax.rem(me, 2)
    chip = me // 2
    col = lax.rem(chip, COLS)
    base = chip - col

    def exists(offset):
        return (chip + offset >= 0) & (chip + offset < chips)

    left = base + lax.rem(col + COLS - 1, COLS)
    right = base + lax.rem(col + 1, COLS)
    sibling = me + 1 - 2 * core

    def core_of(c, k):
        return {"snp": c * 2 + k}

    barrier = pltpu.get_barrier_semaphore()

    first = me == 0

    def greet(c):
        @pl.when(~first)
        def _():
            for k in range(2):
                pl.semaphore_signal(barrier, inc=1, device_id=core_of(c, k), device_id_type=MESH)

    def greets(c):
        return 2 - ((c == 0) & ~first).astype(jnp.int32)

    @pl.when(~first)
    def _():
        pl.semaphore_signal(barrier, inc=1, device_id={"snp": sibling}, device_id_type=MESH)
    greet(left)
    greet(right)
    greeted = greets(left) + greets(right) + (me != 1).astype(jnp.int32)
    for offset in (COLS, -COLS, 1, -1, 2, -2, 3, -3):
        @pl.when(exists(offset))
        def _(offset=offset):
            greet(chip + offset)
        greeted = greeted + greets(chip + offset) * exists(offset).astype(jnp.int32)

    loads = []
    for e in range(2):
        half = core if e == 0 else 1 - core
        for j in range(parts):
            lane = pl.multiple_of((half * parts + j) * LANES, LANES)
            dst = buf.at[OWN, 0, j] if e == 0 else xbuf.at[j]
            loads.append(pltpu.make_async_copy(geno.at[:, pl.ds(lane, LANES)], dst, load_sem.at[e, j]))
            loads[-1].start()

    pos_load = pltpu.make_async_copy(pos_hbm, pos, pos_sem)
    pos_load.start()

    def own_piece(e, j):
        return buf.at[OWN, 0, j] if e == 0 else xbuf.at[j]


    sends_left = col >= 1
    sends_right = (col == 0) | (col == 3)
    uses_lr = col <= 2
    top = chip < COLS
    lag = jnp.where(top, parts + 1, 0)
    late_end = top & (col == 3)
    dz_rl = jnp.where(col == 3, -1, 1)
    dz_lr = jnp.where(col == 0, 1, -1)
    off_rl = jnp.where(col == 3, -2, 1)
    off_lr = jnp.where(col == 0, 3, jnp.where(col == 1, -1, -2))
    off_zrl = off_rl - COLS * dz_rl
    off_zlr = off_lr - COLS * dz_lr

    def offset_of(s):
        return jnp.where(s == RL, off_rl, jnp.where(s == LR, off_lr, jnp.where(s == ZRL, off_zrl, off_zlr)))

    z_rl = exists(-COLS * dz_rl)
    z_lr = exists(-COLS * dz_lr)

    def uses(s):
        along = jnp.where((s == RL) | (s == ZRL), col >= 1, col <= 2)
        return along & ((s < ZRL) | jnp.where(s == ZRL, z_rl, z_lr))

    for copy in loads:
        copy.wait()
    pos_load.wait()
    missing = jnp.zeros((rows, LANES), jnp.int32)
    dosage = jnp.zeros((rows, LANES), jnp.int32)
    for e in range(2):
        for j in range(parts):
            word = own_piece(e, j)[...]
            low = word & 0x55555555
            high = lax.shift_right_logical(word, 1) & 0x55555555
            gone = lax.population_count(low & high)
            missing = missing + gone
            dosage = dosage + lax.population_count(low) + 2 * lax.population_count(high) - 3 * gone
    counts = []
    for x in (missing, dosage):
        total = jnp.broadcast_to(jnp.sum(x, axis=1, keepdims=True), (rows, LANES))
        counts.append(total.T[0:1])
    meta_out[0:1] = pos[...]
    meta_out[1:2] = counts[0]
    meta_out[2:3] = counts[1]
    meta_out[3:8] = jnp.zeros((5, LANES), jnp.int32)

    def fill_tables(s, e, counts8):
        place_of[s, e] = jnp.broadcast_to(counts8.T[:, 0:1], (rows, LANES))
        for i, v in enumerate(values_of(counts8[1:2], counts8[2:3], samples)):
            lane_val[i:i + 1] = v
        columns = lane_val[...].T
        for i in range(3):
            tab[s, e, i] = jnp.broadcast_to(columns[:, i:i + 1], (rows, LANES)).astype(jnp.bfloat16)

    def lanes_of(e, counts8):
        for i, v in enumerate(values_of(counts8[1:2], counts8[2:3], samples)):
            lane_tab[e, i] = jnp.broadcast_to(v, (GROUP, LANES)).astype(jnp.bfloat16)

    def halves_of(word):
        return word.astype(I16), lax.shift_right_logical(word, 16).astype(I16)

    def turn(e, j):
        turned = buf[OWN, e, j].T
        v0, v1, v2 = (lane_tab[e, i] for i in range(3))
        zero = jnp.zeros_like(v0)
        for g in range(0, LANES, GROUP):
            halves = halves_of(turned[g:g + GROUP])
            for q in range(CODES):
                own_t[j, q * LANES + g:q * LANES + g + GROUP, e * rows:(e + 1) * rows] = lookup(
                    halves[q // 8], 2 * (q % 8), v0, v1, v2, zero)

    lane_val[...] = jnp.zeros_like(lane_val)
    fill_tables(OWN, 0, meta_out[...])
    lanes_of(0, meta_out[...])

    def turn_own(j, carry):
        turn(0, j)
        return carry

    lax.fori_loop(0, parts, turn_own, 0)
    pl.semaphore_wait(barrier, greeted)

    @pl.when(first)
    def _():
        pl.semaphore_signal(late_sem, inc=1, device_id={"snp": sibling}, device_id_type=MESH)
        for c in range(1, COLS):
            for k in range(2):
                pl.semaphore_signal(late_sem, inc=1, device_id=core_of(c, k), device_id_type=MESH)

    def meta_copy(offset, e):
        k = core if e == 0 else 1 - core
        return pltpu.make_async_remote_copy(
            src_ref=meta_out, dst_ref=meta_in.at[3 - offset, e], send_sem=meta_send.at[3 + offset, e],
            recv_sem=meta_recv.at[3 - offset, e],
            device_id={"snp": sibling} if offset == 0 else core_of(chip + offset, k), device_id_type=MESH)

    for offset, cols in OWNERS:
        waits = late_end if offset == -3 else False

        @pl.when(any_of(col, cols) & exists(offset) & ~jnp.bool_(waits))
        def _(offset=offset):
            for e in range(2):
                meta_copy(offset, e).start()

    def hop(src, send_sem, s, e, j, target):
        return pltpu.make_async_remote_copy(
            src_ref=src, dst_ref=buf.at[s, e, j], send_sem=send_sem, recv_sem=arrive.at[s, e, j],
            device_id=target, device_id_type=MESH)

    def x_hop(e, j, way):
        c = jnp.where(col == 1, base + 3, left) if way == RL else right
        return hop(own_piece(e, j), x_send.at[way, e, j], way, e, j, core_of(c, core if e == 0 else 1 - core))

    def x_hop_down(e, j):
        return hop(own_piece(e, j), fwd_send.at[LR, e, j], ZLR, e, j,
                   core_of(chip + 1, core if e == 0 else 1 - core))

    def to_first(e, way):
        return late_end & (core == e) if way == LR else False

    def to_sibling(j):
        return hop(xbuf.at[j], sib_send.at[j], OWN, 1, j, {"snp": sibling})

    def greet_sibling():
        meta_copy(0, 1).start()
        for j in range(parts):
            to_sibling(j).start()

    @pl.when(me != 1)
    def _():
        greet_sibling()

    for way, sends in ((RL, sends_left), (LR, sends_right)):
        for j in range(parts):
            for e in range(2):
                @pl.when(sends & ~jnp.bool_(to_first(e, way)))
                def _(way=way, e=e, j=j):
                    x_hop(e, j, way).start()

    @pl.when(late_end)
    def _():
        for j in range(parts):
            for e in range(2):
                x_hop_down(e, j).start()

    out[...] = jnp.zeros_like(out)

    def batch(s, j):
        for e in range(2):
            for g in range(0, rows, GROUP):
                halves = halves_of(buf[s, e, j, g:g + GROUP])
                v0, v1, v2 = (tab[s, e, i, g:g + GROUP] for i in range(3))
                zero = jnp.zeros_like(v0)
                for q in range(CODES):
                    panel[e * rows + g:e * rows + g + GROUP, q * LANES:(q + 1) * LANES] = lookup(
                        halves[q // 8], 2 * (q % 8), v0, v1, v2, zero)
        product = lax.dot_general(panel[...], own_t[j], (((1,), (0,)), ((), ())),
                                  preferred_element_type=jnp.float32)
        for e in range(2):
            for c in range(2):
                tile = product[e * rows:(e + 1) * rows, c * LANES:(c + 1) * LANES]
                acc[s, e, c] = jnp.where(j == 0, tile, acc[s, e, c] + tile)

    def meta_arrived(slot, e):
        pltpu.make_async_remote_copy(
            src_ref=meta_out, dst_ref=meta_in.at[slot, e], send_sem=meta_send.at[slot, e],
            recv_sem=meta_recv.at[slot, e], device_id={"snp": sibling}, device_id_type=MESH).wait_recv()

    @pl.when(me == 1)
    def _():
        pl.semaphore_wait(late_sem, 1)
        greet_sibling()

    meta_arrived(3, 1)
    fill_tables(OWN, 1, meta_in[3, 1])
    lanes_of(1, meta_in[3, 1])

    def part_copy(s, e):
        return pltpu.make_async_remote_copy(
            src_ref=acc.at[s, e, 1], dst_ref=part.at[s, 1 - e], send_sem=part_send.at[s, e],
            recv_sem=part_recv.at[s, 1 - e], device_id={"snp": sibling}, device_id_type=MESH)

    def part_arrived(s, e):
        pltpu.make_async_remote_copy(
            src_ref=acc.at[s, e, 1], dst_ref=part.at[s, e], send_sem=part_send.at[s, e],
            recv_sem=part_recv.at[s, e], device_id={"snp": sibling}, device_id_type=MESH).wait_recv()

    def own_step(j):
        to_sibling(j).wait_recv()
        turn(1, j)
        batch(OWN, j)

        @pl.when(j == parts - 1)
        def _():
            for e in range(2):
                part_copy(OWN, e).start()

    passes_rl = (col >= 1) & exists(COLS * dz_rl)
    passes_lr = uses_lr & exists(COLS * dz_lr) & (chip > 0)

    def fwd_rl(e, j):
        return hop(buf.at[RL, e, j], fwd_send.at[RL, e, j], ZRL, e, j, core_of(chip + COLS * dz_rl, core))

    def fwd_lr(e, j):
        return hop(buf.at[LR, e, j], fwd_send.at[LR, e, j], ZLR, e, j, core_of(chip + COLS * dz_lr, core))

    def fwd_lr_on(e, j):
        return hop(buf.at[LR, e, j], fwd2_send.at[e, j], LR, e, j, core_of(right, core))

    def arrived(s, e, j):
        hop(buf.at[s, e, j], fwd_send.at[RL, e, j], s, e, j, {"snp": sibling}).wait_recv()

    def put(tile, at):
        @pl.when((at >= 0) & (at <= 2 * REACH))
        def _():
            out[:, pl.ds(pl.multiple_of(at * LANES, LANES), LANES)] = tile

    def finished(s, e):
        part_arrived(s, e)
        tile = (acc[s, e, 0] + part[s, e]) / samples
        near = jnp.abs(place_of[s, e] - pos[...]) <= BAND_BP
        return jnp.where(near, tile, jnp.zeros_like(tile))

    def mirror_copy(s, e, offset):
        k = core if e == 0 else 1 - core
        return pltpu.make_async_remote_copy(
            src_ref=mir_out.at[s, e], dst_ref=mir_in.at[3 - offset, e], send_sem=mir_send.at[s, e],
            recv_sem=mir_recv.at[3 - offset, e], device_id=core_of(chip + offset, k), device_id_type=MESH)

    def column_of(offset, e):
        k = core if e == 0 else 1 - core
        return 2 * (offset + 3) + k - core

    def finish(s):
        offset = offset_of(s)
        for e in range(2):
            tile = finished(s, e)
            mir_out[s, e] = tile.astype(jnp.bfloat16)
            mirror_copy(s, e, offset).start()
            put(tile.T, column_of(offset, e))

    def finish_some(low, high, wanted):
        def one(s, carry):
            @pl.when(wanted(s) & uses(s))
            def _():
                finish(s)
            return carry

        lax.fori_loop(low, high, one, 0)

    def step(t, carry):
        @pl.when((t == parts + 1) & (col >= 1))
        def _():
            pl.semaphore_wait(late_sem, 1)

            @pl.when(late_end)
            def _():
                for e in range(2):
                    meta_copy(-3, e).start()
                for j in range(parts):
                    for e in range(2):
                        @pl.when(to_first(e, LR))
                        def _(e=e, j=j):
                            x_hop(e, j, LR).start()

        behind = t - lag
        for e in range(2):
            @pl.when((t >= 0) & (t < parts) & (col >= 1))
            def _(e=e):
                arrived(RL, e, t)

                @pl.when(passes_rl)
                def _():
                    fwd_rl(e, t).start()

            @pl.when((behind >= 0) & (behind < parts) & uses_lr)
            def _(e=e):
                arrived(LR, e, behind)

                @pl.when(col == 1)
                def _():
                    fwd_lr_on(e, behind).start()

                @pl.when(passes_lr)
                def _():
                    fwd_lr(e, behind).start()

        @pl.when(t < parts - 1)
        def _():
            own_step(t + 1)

        @pl.when(t == parts)
        def _():
            finish_some(RL, ZRL, lambda s: (s == RL) | (lag == 0))
            for e in range(2):
                put(finished(OWN, e).T, column_of(0, e))

        @pl.when(t == parts + 1)
        def _():
            finish_some(ZRL, OWN, lambda s: s >= ZRL)

        def stream(s, inner):
            j = jnp.where(s >= ZRL, t - 1, jnp.where(s == LR, behind, t))

            @pl.when(uses(s) & (j >= 0) & (j < parts))
            def _():
                @pl.when(j == 0)
                def _():
                    slot = offset_of(s) + 3
                    for e in range(2):
                        meta_arrived(slot, e)
                        fill_tables(s, e, meta_in[slot, e])

                @pl.when(s >= ZRL)
                def _():
                    for e in range(2):
                        arrived(s, e, j)
                batch(s, j)

                @pl.when(j == parts - 1)
                def _():
                    for e in range(2):
                        part_copy(s, e).start()
            return inner

        lax.fori_loop(RL, OWN, stream, 0)
        return carry

    lax.fori_loop(-1, parts + 1 + lag, step, 0)
    finish_some(RL, OWN, lambda s: jnp.where(lag == 0, s >= ZRL, s == LR))

    for offset, cols in OWNERS:
        @pl.when(any_of(col, cols) & exists(offset))
        def _(offset=offset):
            for e in range(2):
                pltpu.make_async_remote_copy(
                    src_ref=mir_out.at[0, e], dst_ref=mir_in.at[3 + offset, e], send_sem=mir_send.at[0, e],
                    recv_sem=mir_recv.at[3 + offset, e], device_id={"snp": sibling},
                    device_id_type=MESH).wait_recv()
                put(mir_in[3 + offset, e].astype(jnp.float32), column_of(offset, e))

    for way, sends in ((RL, sends_left), (LR, sends_right)):
        @pl.when(sends)
        def _(way=way):
            for j in range(parts):
                for e in range(2):
                    x_hop(e, j, way).wait_send()
    for j in range(parts):
        to_sibling(j).wait_send()

    @pl.when(passes_rl)
    def _():
        for j in range(parts):
            for e in range(2):
                fwd_rl(e, j).wait_send()

    @pl.when(passes_lr | late_end)
    def _():
        for j in range(parts):
            for e in range(2):
                fwd_lr(e, j).wait_send()

    @pl.when(col == 1)
    def _():
        for j in range(parts):
            for e in range(2):
                fwd_lr_on(e, j).wait_send()
    meta_copy(0, 1).wait_send()
    for offset, cols in OWNERS:
        @pl.when(any_of(col, cols) & exists(offset))
        def _(offset=offset):
            for e in range(2):
                meta_copy(offset, e).wait_send()
    for e in range(2):
        part_copy(OWN, e).wait_send()

    def drain(s, carry):
        @pl.when(uses(s))
        def _():
            for e in range(2):
                part_copy(s, e).wait_send()
                mirror_copy(s, e, offset_of(s)).wait_send()
        return carry

    lax.fori_loop(0, 4, drain, 0)


def per_device(genotypes, positions):
    devices = lax.axis_size("snp")
    rows, words = genotypes.shape
    parts = words // (2 * LANES)
    piece = (rows, LANES)
    dma = pltpu.SemaphoreType.DMA
    return pl.pallas_call(
        functools.partial(kernel, devices),
        out_shape=pltpu.VMEM((rows, (2 * REACH + 1) * LANES), jnp.float32),
        in_specs=[pl.BlockSpec(memory_space=pltpu.HBM)] * 2,
        out_specs=pl.BlockSpec(memory_space=pltpu.VMEM),
        scratch_shapes=[
            pltpu.VMEM((1, rows), jnp.int32),
            pltpu.VMEM((5, 2, parts) + piece, jnp.int32),
            pltpu.VMEM((parts,) + piece, jnp.int32),
            pltpu.VMEM((parts, CODES * LANES, 2 * rows), jnp.bfloat16),
            pltpu.VMEM((2 * rows, CODES * LANES), jnp.bfloat16),
            pltpu.VMEM((5, 2, 2) + piece, jnp.float32),
            pltpu.VMEM((5, 2) + piece, jnp.float32),
            pltpu.VMEM((5, 2, 3) + piece, jnp.bfloat16),
            pltpu.VMEM((5, 2) + piece, jnp.int32),
            pltpu.VMEM((2, 3, GROUP, LANES), jnp.bfloat16),
            pltpu.VMEM((8, LANES), jnp.int32),
            pltpu.VMEM((7, 2, 8, LANES), jnp.int32),
            pltpu.VMEM((4, 2) + piece, jnp.bfloat16),
            pltpu.VMEM((7, 2) + piece, jnp.bfloat16),
            pltpu.VMEM((8, LANES), jnp.float32),
            pltpu.SemaphoreType.REGULAR,
            dma((2, parts)),
            dma,
            dma((2, 2, parts)),
            dma((2, 2, parts)),
            dma((2, parts)),
            dma((5, 2, parts)),
            dma((7, 2)),
            dma((7, 2)),
            dma((parts,)),
            dma((5, 2)),
            dma((5, 2)),
            dma((4, 2)),
            dma((7, 2)),
        ],
        compiler_params=pltpu.CompilerParams(
            collective_id=0, has_side_effects=True, vmem_limit_bytes=60 * 1024 * 1024
        ),
    )(genotypes, positions.reshape(1, rows))


def solution(mesh):
    return jax.shard_map(
        per_device,
        mesh=mesh,
        in_specs=(P(("arm", "snp"), None), P(("arm", "snp"))),
        out_specs=P(("arm", "snp"), None),
        check_vma=False,
    )
```

time: 73 us -> 52.2 us (0.72)
  Pallas kernels: 70.2 us -> 51.2 us
  local copies, waits for them, and re-layouts: 2.6 us -> 0.9 us
    pallas_call x1, Pallas kernels: 70.2 us -> 51.2 us  [per_device(): pl.pallas_call(functools.partial(kernel, devices), out_shape=pltpu.VMEM((...]
    unnamed x5 -> x1, local copies, waits for them, and re-layouts: 2.6 us -> 0.9 us
where the time goes in v1:
time: 52.2 us; the launch traced here: 52.1 us
  Pallas kernels  51.2 us (98%)
  local copies, waits for them, and re-layouts  0.9 us (2%)
    pallas_call x1, Pallas kernels, per_device(): pl.pallas_call(functools.partial(kernel, devices), out_shape=pltpu.VMEM((...  51.2 us

profile of v1, /device:TPU:33, one launch (start us, length us, event | category | flops | bytes accessed | tf_op | source)
XLA Modules:
  0.0 52.1 jit_solution(7547672338154939202)
XLA Ops:
  0.0 51.2 %shard_map.28 = f32[128,1664]{1,0:T(8,128)S(1)} custom-call(s32[128,1024]{1,0:T(8,128)} %geno.1, s32[1,128]{1,0:T(1,128)} %bitcast.1), custom_call_target="tpu_custom_call" | custom-call | tf_op jit(solution)/shard_map/pallas_call | solution.py:501
  51.2 0.9 %copy.4 = f32[128,1664]{1,0:T(8,128)} copy(f32[128,1664]{1,0:T(8,128)S(1)} %shard_map.28) | data formatting | bytes 1703936

commit v2 on v1

--- a/solution.py
+++ b/solution.py
@@ -16,7 +16,7 @@
 MESH = pl.DeviceIdType.MESH
 I16 = jnp.int16
 GROUP = 16
-OWNERS = ((1, (0, 3)), (-1, (2, 3)), (2, (0, 1)), (-2, (0, 1)), (3, (2, 3)), (-3, (0, 3)))
+OWNERS = ((1, (0, 3)), (2, (0, 1)), (3, (2, 3)), (-2, (0, 1)), (-1, (2, 3)), (-3, (0, 3)))
 
 
 def any_of(col, cols):
@@ -58,6 +58,12 @@
     def exists(offset):
         return (chip + offset >= 0) & (chip + offset < chips)
 
+    def owned_at(offset, cols):
+        there = any_of(col, cols)
+        if offset == 1:
+            return there & (chip > 0)
+        return there | (chip == 1) if offset == -1 else there
+
     left = base + lax.rem(col + COLS - 1, COLS)
     right = base + lax.rem(col + 1, COLS)
     sibling = me + 1 - 2 * core
@@ -108,10 +114,17 @@
 
     sends_left = col >= 1
     sends_right = (col == 0) | (col == 3)
-    uses_lr = col <= 2
+    uses_rl = (col >= 1) | (chip == 0)
+    uses_lr = (col <= 2) & (chip != 1)
     top = chip < COLS
-    lag = jnp.where(top, parts + 1, 0)
-    late_end = top & (col == 3)
+
+    def lag_of(s):
+        late = jnp.where(top, parts + 1, jnp.where(col == 2, 1, 0))
+        return jnp.where(s == RL, jnp.where(chip == 0, parts + 1, 0), jnp.where(s == LR, late, jnp.where((s == ZLR) & (col == 2), 2, 1)))
+
+    lag = lag_of(LR)
+    steps = parts + 1 + jnp.where(top, parts + 1, jnp.where(col == 2, 2, 1))
+    late_end = (chip == 1) | (chip == 3)
     dz_rl = jnp.where(col == 3, -1, 1)
     dz_lr = jnp.where(col == 0, 1, -1)
     off_rl = jnp.where(col == 3, -2, 1)
@@ -126,8 +139,8 @@
     z_lr = exists(-COLS * dz_lr)
 
     def uses(s):
-        along = jnp.where((s == RL) | (s == ZRL), col >= 1, col <= 2)
-        return along & ((s < ZRL) | jnp.where(s == ZRL, z_rl, z_lr))
+        z = jnp.where(s == ZRL, z_rl & (col >= 1), z_lr & (col <= 2))
+        return jnp.where(s == RL, uses_rl, jnp.where(s == LR, uses_lr, z))
 
     for copy in loads:
         copy.wait()
@@ -151,6 +164,81 @@
     meta_out[2:3] = counts[1]
     meta_out[3:8] = jnp.zeros((5, LANES), jnp.int32)
 
+    def meta_copy(offset, e):
+        k = core if e == 0 else 1 - core
+        return pltpu.make_async_remote_copy(
+            src_ref=meta_out, dst_ref=meta_in.at[3 - offset, e], send_sem=meta_send.at[3 + offset, e],
+            recv_sem=meta_recv.at[3 - offset, e],
+            device_id={"snp": sibling} if offset == 0 else core_of(chip + offset, k), device_id_type=MESH)
+
+    def hop(src, send_sem, s, e, j, target):
+        return pltpu.make_async_remote_copy(
+            src_ref=src, dst_ref=buf.at[s, e, j], send_sem=send_sem, recv_sem=arrive.at[s, e, j],
+            device_id=target, device_id_type=MESH)
+
+    def x_hop(e, j, way):
+        c = jnp.where(col == 1, base + 3, left) if way == RL else jnp.where(chip == 0, 2, right)
+        return hop(own_piece(e, j), x_send.at[way, e, j], way, e, j, core_of(c, core if e == 0 else 1 - core))
+
+    def x_hop_down(e, j):
+        return hop(own_piece(e, j), fwd_send.at[LR, e, j], ZLR, e, j,
+                   core_of(chip + 1, core if e == 0 else 1 - core))
+
+    def to_first(e, way):
+        return (chip == 3) & (core == e) if way == LR else False
+
+    def x_hop_first(e, j):
+        return hop(own_piece(e, j), x_send.at[LR, e, j], RL, e, j, core_of(0, core if e == 0 else 1 - core))
+
+    def to_sibling(j):
+        return hop(xbuf.at[j], sib_send.at[j], OWN, 1, j, {"snp": sibling})
+
+    def greet_sibling():
+        meta_copy(0, 1).start()
+        for j in range(parts):
+            to_sibling(j).start()
+
+    def send_first():
+        for offset, cols in OWNERS:
+            waits = chip + offset == 0 if offset in (-1, -3) else False
+
+            @pl.when(owned_at(offset, cols) & exists(offset) & ~jnp.bool_(waits))
+            def _(offset=offset):
+                for e in range(2):
+                    meta_copy(offset, e).start()
+
+        @pl.when(me != 1)
+        def _():
+            greet_sibling()
+
+        for way, sends in ((RL, sends_left), (LR, sends_right)):
+            for j in range(parts):
+                for e in range(2):
+                    @pl.when(sends & ~jnp.bool_(to_first(e, way)))
+                    def _(way=way, e=e, j=j):
+                        x_hop(e, j, way).start()
+
+        @pl.when(chip == 3)
+        def _():
+            for j in range(parts):
+                for e in range(2):
+                    x_hop_down(e, j).start()
+
+        for e in range(2):
+            @pl.when((chip == 1) & (core != e))
+            def _(e=e):
+                for j in range(parts):
+                    x_hop_first(e, j).start()
+
+    @pl.when(first)
+    def _():
+        pl.semaphore_wait(barrier, greeted)
+        pl.semaphore_signal(late_sem, inc=1, device_id={"snp": sibling}, device_id_type=MESH)
+        for c in range(1, COLS):
+            for k in range(2):
+                pl.semaphore_signal(late_sem, inc=1, device_id=core_of(c, k), device_id_type=MESH)
+        send_first()
+
     def fill_tables(s, e, counts8):
         place_of[s, e] = jnp.broadcast_to(counts8.T[:, 0:1], (rows, LANES))
         for i, v in enumerate(values_of(counts8[1:2], counts8[2:3], samples)):
@@ -177,6 +265,7 @@
                     halves[q // 8], 2 * (q % 8), v0, v1, v2, zero)
 
     lane_val[...] = jnp.zeros_like(lane_val)
+    acc[...] = jnp.zeros_like(acc)
     fill_tables(OWN, 0, meta_out[...])
     lanes_of(0, meta_out[...])
 
@@ -185,70 +274,10 @@
         return carry
 
     lax.fori_loop(0, parts, turn_own, 0)
-    pl.semaphore_wait(barrier, greeted)
-
-    @pl.when(first)
-    def _():
-        pl.semaphore_signal(late_sem, inc=1, device_id={"snp": sibling}, device_id_type=MESH)
-        for c in range(1, COLS):
-            for k in range(2):
-                pl.semaphore_signal(late_sem, inc=1, device_id=core_of(c, k), device_id_type=MESH)
-
-    def meta_copy(offset, e):
-        k = core if e == 0 else 1 - core
-        return pltpu.make_async_remote_copy(
-            src_ref=meta_out, dst_ref=meta_in.at[3 - offset, e], send_sem=meta_send.at[3 + offset, e],
-            recv_sem=meta_recv.at[3 - offset, e],
-            device_id={"snp": sibling} if offset == 0 else core_of(chip + offset, k), device_id_type=MESH)
-
-    for offset, cols in OWNERS:
-        waits = late_end if offset == -3 else False
-
-        @pl.when(any_of(col, cols) & exists(offset) & ~jnp.bool_(waits))
-        def _(offset=offset):
-            for e in range(2):
-                meta_copy(offset, e).start()
-
-    def hop(src, send_sem, s, e, j, target):
-        return pltpu.make_async_remote_copy(
-            src_ref=src, dst_ref=buf.at[s, e, j], send_sem=send_sem, recv_sem=arrive.at[s, e, j],
-            device_id=target, device_id_type=MESH)
-
-    def x_hop(e, j, way):
-        c = jnp.where(col == 1, base + 3, left) if way == RL else right
-        return hop(own_piece(e, j), x_send.at[way, e, j], way, e, j, core_of(c, core if e == 0 else 1 - core))
-
-    def x_hop_down(e, j):
-        return hop(own_piece(e, j), fwd_send.at[LR, e, j], ZLR, e, j,
-                   core_of(chip + 1, core if e == 0 else 1 - core))
-
-    def to_first(e, way):
-        return late_end & (core == e) if way == LR else False
-
-    def to_sibling(j):
-        return hop(xbuf.at[j], sib_send.at[j], OWN, 1, j, {"snp": sibling})
-
-    def greet_sibling():
-        meta_copy(0, 1).start()
-        for j in range(parts):
-            to_sibling(j).start()
-
-    @pl.when(me != 1)
-    def _():
-        greet_sibling()
-
-    for way, sends in ((RL, sends_left), (LR, sends_right)):
-        for j in range(parts):
-            for e in range(2):
-                @pl.when(sends & ~jnp.bool_(to_first(e, way)))
-                def _(way=way, e=e, j=j):
-                    x_hop(e, j, way).start()
-
-    @pl.when(late_end)
-    def _():
-        for j in range(parts):
-            for e in range(2):
-                x_hop_down(e, j).start()
+    @pl.when(~first)
+    def _():
+        pl.semaphore_wait(barrier, greeted)
+        send_first()
 
     out[...] = jnp.zeros_like(out)
 
@@ -266,7 +295,7 @@
         for e in range(2):
             for c in range(2):
                 tile = product[e * rows:(e + 1) * rows, c * LANES:(c + 1) * LANES]
-                acc[s, e, c] = jnp.where(j == 0, tile, acc[s, e, c] + tile)
+                acc[s, e, c] += tile
 
     def meta_arrived(slot, e):
         pltpu.make_async_remote_copy(
@@ -304,6 +333,7 @@
 
     passes_rl = (col >= 1) & exists(COLS * dz_rl)
     passes_lr = uses_lr & exists(COLS * dz_lr) & (chip > 0)
+    passes_on = (col == 1) & (chip != 1)
 
     def fwd_rl(e, j):
         return hop(buf.at[RL, e, j], fwd_send.at[RL, e, j], ZRL, e, j, core_of(chip + COLS * dz_rl, core))
@@ -346,45 +376,44 @@
             mirror_copy(s, e, offset).start()
             put(tile.T, column_of(offset, e))
 
-    def finish_some(low, high, wanted):
-        def one(s, carry):
-            @pl.when(wanted(s) & uses(s))
-            def _():
-                finish(s)
-            return carry
-
-        lax.fori_loop(low, high, one, 0)
-
     def step(t, carry):
-        @pl.when((t == parts + 1) & (col >= 1))
+        @pl.when(top & (col >= 1) & (t == parts))
         def _():
             pl.semaphore_wait(late_sem, 1)
 
-            @pl.when(late_end)
-            def _():
-                for e in range(2):
-                    meta_copy(-3, e).start()
-                for j in range(parts):
+            for offset in (-1, -3):
+                @pl.when(late_end & (chip + offset == 0))
+                def _(offset=offset):
                     for e in range(2):
-                        @pl.when(to_first(e, LR))
-                        def _(e=e, j=j):
-                            x_hop(e, j, LR).start()
+                        meta_copy(offset, e).start()
+            for e in range(2):
+                @pl.when((chip == 1) & (core == e))
+                def _(e=e):
+                    for j in range(parts):
+                        x_hop_first(e, j).start()
+
+                @pl.when((chip == 3) & (core == e))
+                def _(e=e):
+                    for j in range(parts):
+                        x_hop(e, j, LR).start()
 
         behind = t - lag
         for e in range(2):
-            @pl.when((t >= 0) & (t < parts) & (col >= 1))
-            def _(e=e):
-                arrived(RL, e, t)
+            at_rl = t - lag_of(RL)
+
+            @pl.when((at_rl >= 0) & (at_rl < parts) & uses_rl)
+            def _(e=e, at_rl=at_rl):
+                arrived(RL, e, at_rl)
 
                 @pl.when(passes_rl)
                 def _():
-                    fwd_rl(e, t).start()
+                    fwd_rl(e, at_rl).start()
 
             @pl.when((behind >= 0) & (behind < parts) & uses_lr)
             def _(e=e):
                 arrived(LR, e, behind)
 
-                @pl.when(col == 1)
+                @pl.when(passes_on)
                 def _():
                     fwd_lr_on(e, behind).start()
 
@@ -398,16 +427,11 @@
 
         @pl.when(t == parts)
         def _():
-            finish_some(RL, ZRL, lambda s: (s == RL) | (lag == 0))
             for e in range(2):
                 put(finished(OWN, e).T, column_of(0, e))
 
-        @pl.when(t == parts + 1)
-        def _():
-            finish_some(ZRL, OWN, lambda s: s >= ZRL)
-
         def stream(s, inner):
-            j = jnp.where(s >= ZRL, t - 1, jnp.where(s == LR, behind, t))
+            j = t - lag_of(s)
 
             @pl.when(uses(s) & (j >= 0) & (j < parts))
             def _():
@@ -428,16 +452,19 @@
                 def _():
                     for e in range(2):
                         part_copy(s, e).start()
+
+            @pl.when(uses(s) & (j == parts))
+            def _():
+                finish(s)
             return inner
 
         lax.fori_loop(RL, OWN, stream, 0)
         return carry
 
-    lax.fori_loop(-1, parts + 1 + lag, step, 0)
-    finish_some(RL, OWN, lambda s: jnp.where(lag == 0, s >= ZRL, s == LR))
+    lax.fori_loop(-1, steps, step, 0)
 
     for offset, cols in OWNERS:
-        @pl.when(any_of(col, cols) & exists(offset))
+        @pl.when(owned_at(offset, cols) & exists(offset))
         def _(offset=offset):
             for e in range(2):
                 pltpu.make_async_remote_copy(
@@ -446,7 +473,7 @@
                     device_id_type=MESH).wait_recv()
                 put(mir_in[3 + offset, e].astype(jnp.float32), column_of(offset, e))
 
-    for way, sends in ((RL, sends_left), (LR, sends_right)):
+    for way, sends in ((RL, sends_left), (LR, sends_right | (chip == 1))):
         @pl.when(sends)
         def _(way=way):
             for j in range(parts):
@@ -461,20 +488,20 @@
             for e in range(2):
                 fwd_rl(e, j).wait_send()
 
-    @pl.when(passes_lr | late_end)
+    @pl.when(passes_lr | (chip == 3))
     def _():
         for j in range(parts):
             for e in range(2):
                 fwd_lr(e, j).wait_send()
 
-    @pl.when(col == 1)
+    @pl.when(passes_on)
     def _():
         for j in range(parts):
             for e in range(2):
                 fwd_lr_on(e, j).wait_send()
     meta_copy(0, 1).wait_send()
     for offset, cols in OWNERS:
-        @pl.when(any_of(col, cols) & exists(offset))
+        @pl.when(owned_at(offset, cols) & exists(offset))
         def _(offset=offset):
             for e in range(2):
                 meta_copy(offset, e).wait_send()

time: 52.2 us -> 44.3 us (0.85)
  Pallas kernels: 51.2 us -> 43.2 us
    pallas_call x1, Pallas kernels: 51.2 us -> 43.2 us  [per_device(): pl.pallas_call(functools.partial(kernel, devices), out_shape=pltpu.VMEM((...]
where the time goes in v2:
time: 44.3 us; the launch traced here: 44.1 us
  Pallas kernels  43.2 us (98%)
  local copies, waits for them, and re-layouts  0.9 us (2%)
    pallas_call x1, Pallas kernels, per_device(): pl.pallas_call(functools.partial(kernel, devices), out_shape=pltpu.VMEM((...  43.2 us
    unnamed x1, local copies, waits for them, and re-layouts  0.9 us

profile of v2, /device:TPU:33, one launch (start us, length us, event | category | flops | bytes accessed | tf_op | source)
XLA Modules:
  0.0 44.1 jit_solution(10876870603659731710)
XLA Ops:
  0.0 43.2 %shard_map.28 = f32[128,1664]{1,0:T(8,128)S(1)} custom-call(s32[128,1024]{1,0:T(8,128)} %geno.1, s32[1,128]{1,0:T(1,128)} %bitcast.1), custom_call_target="tpu_custom_call" | custom-call | tf_op jit(solution)/shard_map/pallas_call | solution.py:528
  43.2 0.9 %copy.4 = f32[128,1664]{1,0:T(8,128)} copy(f32[128,1664]{1,0:T(8,128)S(1)} %shard_map.28) | data formatting | bytes 1703936

commit v3 on v2

--- a/solution.py
+++ b/solution.py
@@ -463,16 +463,6 @@
 
     lax.fori_loop(-1, steps, step, 0)
 
-    for offset, cols in OWNERS:
-        @pl.when(owned_at(offset, cols) & exists(offset))
-        def _(offset=offset):
-            for e in range(2):
-                pltpu.make_async_remote_copy(
-                    src_ref=mir_out.at[0, e], dst_ref=mir_in.at[3 + offset, e], send_sem=mir_send.at[0, e],
-                    recv_sem=mir_recv.at[3 + offset, e], device_id={"snp": sibling},
-                    device_id_type=MESH).wait_recv()
-                put(mir_in[3 + offset, e].astype(jnp.float32), column_of(offset, e))
-
     for way, sends in ((RL, sends_left), (LR, sends_right | (chip == 1))):
         @pl.when(sends)
         def _(way=way):
@@ -517,6 +507,16 @@
         return carry
 
     lax.fori_loop(0, 4, drain, 0)
+
+    for offset, cols in OWNERS:
+        @pl.when(owned_at(offset, cols) & exists(offset))
+        def _(offset=offset):
+            for e in range(2):
+                pltpu.make_async_remote_copy(
+                    src_ref=mir_out.at[0, e], dst_ref=mir_in.at[3 + offset, e], send_sem=mir_send.at[0, e],
+                    recv_sem=mir_recv.at[3 + offset, e], device_id={"snp": sibling},
+                    device_id_type=MESH).wait_recv()
+                put(mir_in[3 + offset, e].astype(jnp.float32), column_of(offset, e))
 
 
 def per_device(genotypes, positions):

time: 44.3 us -> 44.2 us (level)
  no operation moved by 1% of the time
where the time goes in v3:
time: 44.2 us; the launch traced here: 44 us
  Pallas kernels  43.1 us (98%)
  local copies, waits for them, and re-layouts  0.9 us (2%)
    pallas_call x1, Pallas kernels, per_device(): pl.pallas_call(functools.partial(kernel, devices), out_shape=pltpu.VMEM((...  43.1 us
    unnamed x1, local copies, waits for them, and re-layouts  0.9 us

profile of v3, /device:TPU:33, one launch (start us, length us, event | category | flops | bytes accessed | tf_op | source)
XLA Modules:
  0.0 44.0 jit_solution(17102841629303931262)
XLA Ops:
  0.0 43.1 %shard_map.28 = f32[128,1664]{1,0:T(8,128)S(1)} custom-call(s32[128,1024]{1,0:T(8,128)} %geno.1, s32[1,128]{1,0:T(1,128)} %bitcast.1), custom_call_target="tpu_custom_call" | custom-call | tf_op jit(solution)/shard_map/pallas_call | solution.py:528
  43.1 0.9 %copy.4 = f32[128,1664]{1,0:T(8,128)} copy(f32[128,1664]{1,0:T(8,128)S(1)} %shard_map.28) | data formatting | bytes 1703936
